TPU v7x, 128 devices: a whole 4x4x4 slice. The times are simulated.
128 devices in a mesh: dom: 128 (over y, z, x, core).
Axes of the slice: x: 4, y: 4, z: 4, core: 2. Of those that a mesh axis runs over, the one named last changes fastest.
Arguments:
- right_side: float32 [131072, 3], P('dom'), may hold values from -10 to 10
- fine_diagonal: float32 [131072, 3], P('dom'), may hold values from 2 to 4
- fine_columns: int32 [131072, 27], P('dom'), may hold values from 0 to 131071, as said below
- fine_blocks: float32 [131072, 27, 3, 3], P('dom'), may hold values from -0.625 to 0.625
- aggregate_of_node: int32 [131072], P('dom'), may hold values from 0 to 31, as said below
- coarse_row_of_aggregate: int32 [4096], P('dom'), may hold values from 0 to 4095, as said below
- coarse_diagonal: float32 [4096, 3], P('dom'), may hold values from 2 to 4
- coarse_columns: int32 [4096, 27], P('dom'), may hold values from 0 to 4095
- coarse_blocks: float32 [4096, 27, 3, 3], P('dom'), may hold values from -0.625 to 0.625
Outputs:
- solution: float32 [131072, 3], P('dom')
- correction: float32 [4096, 3], P('dom')
Inputs may be any that keep to these rules, and one draw needn't show every extreme that they name: Every entry of fine_columns differs from its row number by at most 256, and some entry by exactly 256. `aggregate_of_node`: on each device every aggregate number 0 to 31 is used by at least one of its nodes. coarse_row_of_aggregate is a permutation of 0 to 4095; among the 32 aggregates of one device (an aligned block of entries) at most 8 get rows of any one owner, and exactly 8 for some owner.
All inputs are finite; a program needn't handle non-finite values.
Results may differ from a plain program's by a relative error of at most 0.0003.
Values sent between devices are 32-bit elements.
A program may use at most 64 MiB of HBM per device.

v0:
```python
import functools

import jax
import jax.numpy as jnp
from jax import lax
from jax.experimental import pallas as pl
from jax.experimental.pallas import tpu as pltpu
from jax.sharding import PartitionSpec as P

WIN = 256
SWEEPS = 2
CSWEEPS = 6
LANES = 128

damping = 0.7


def pick(source, lane):
    return jnp.take_along_axis(source, lane, axis=1, mode="promise_in_bounds")


def fine_kernel(smooth, pad_ref, index_ref, block_ref, diagonal_ref, right_ref, out_ref):
    slots, chunks, _ = index_ref.shape
    margin = WIN // LANES
    sources = [[pad_ref[c, j : j + chunks, :] for j in range(2 * margin + 1)] for c in range(3)]
    total = [jnp.zeros((chunks, LANES), jnp.float32) for _ in range(3)]
    for k in range(slots):
        position = index_ref[k]
        lane, chunk = position & (LANES - 1), position >> 7
        masks = [chunk == j for j in range(2 * margin + 1)]
        for c in range(3):
            near = pick(sources[c][0], lane)
            for j in range(1, 2 * margin + 1):
                near = jnp.where(masks[j], pick(sources[c][j], lane), near)
            for i in range(3):
                total[i] = total[i] + block_ref[k, i, c] * near
    for i in range(3):
        field = pad_ref[i, margin : margin + chunks, :]
        residual = right_ref[i] - (diagonal_ref[i] * field - total[i])
        if smooth:
            out_ref[i] = field + damping * residual / diagonal_ref[i]
        else:
            out_ref[i] = residual


def far_pick(values, position):
    lane, chunk = position & (LANES - 1), position >> 7
    out = []
    for value in values:
        count = value.shape[0]
        near = jnp.zeros(position.shape, jnp.float32)
        for j in range(count):
            row = jnp.broadcast_to(value[j : j + 1, :], position.shape)
            near = jnp.where(chunk == j, pick(row, lane), near)
        out.append(near)
    return out


def coarse_kernel(sums_ref, inverse_ref, column_ref, block_ref, diagonal_ref, label_ref, own_ref, field_ref,
                  out_ref, correction_ref, rhs_ref, next_ref):
    slots, chunks, _ = column_ref.shape
    group = 8
    groups = chunks // group
    for g in range(groups):
        rows = pl.ds(g * group, group)
        picked = far_pick([sums_ref[c] for c in range(3)], inverse_ref[rows, :])
        for c in range(3):
            rhs_ref[c, rows, :] = picked[c]
            correction_ref[c, rows, :] = damping * picked[c] / diagonal_ref[c, rows, :]

    def sweep(_, carry):
        for g in range(groups):
            rows = pl.ds(g * group, group)

            def slot(k, total):
                total = list(total)
                near = far_pick([correction_ref[c] for c in range(3)], column_ref[k, rows, :])
                for i in range(3):
                    for c in range(3):
                        total[i] = total[i] + block_ref[k, i, c, rows, :] * near[c]
                return tuple(total)

            zero = jnp.zeros((group, LANES), jnp.float32)
            total = lax.fori_loop(0, slots, slot, (zero,) * 3, unroll=9 if groups == 1 else 1)
            for i in range(3):
                diagonal, field = diagonal_ref[i, rows, :], correction_ref[i, rows, :]
                residual = rhs_ref[i, rows, :] - (diagonal * field - total[i])
                next_ref[i, rows, :] = field + damping * residual / diagonal
        correction_ref[...] = next_ref[...]
        return carry

    lax.fori_loop(0, CSWEEPS - 1, sweep, 0)
    label = label_ref[...]
    row = pick(jnp.broadcast_to(own_ref[...], label.shape), label)
    picked = far_pick([correction_ref[c] for c in range(3)], row)
    for c in range(3):
        out_ref[c] = field_ref[c] + picked[c]


def per_device(
    right_side,
    fine_diagonal,
    fine_columns,
    fine_blocks,
    aggregate_of_node,
    coarse_row_of_aggregate,
    coarse_diagonal,
    coarse_columns,
    coarse_blocks,
):
    devices, me = lax.axis_size("dom"), lax.axis_index("dom")
    nodes, slots = fine_columns.shape
    chunks, margin = nodes // LANES, WIN // LANES
    own, coarse_slots = coarse_columns.shape
    rows = own * devices
    up = [(i, i + 1) for i in range(devices - 1)]
    down = [(j, i) for i, j in up]

    right = right_side.T.reshape(3, chunks, LANES)
    diagonal = fine_diagonal.T.reshape(3, chunks, LANES)
    blocks = jnp.transpose(fine_blocks, (1, 2, 3, 0)).reshape(slots, 3, 3, chunks, LANES)
    shift = LANES * jnp.arange(chunks, dtype=jnp.int32)[None, :, None]
    index = fine_columns.T.reshape(slots, chunks, LANES) - (me * nodes - WIN) - shift
    label = aggregate_of_node.reshape(chunks, LANES)

    floats = jnp.concatenate(
        [jnp.transpose(coarse_blocks, (1, 2, 3, 0)).reshape(coarse_slots * 9, own), coarse_diagonal.T], axis=0
    )
    integers = jnp.concatenate([coarse_columns.T, coarse_row_of_aggregate[None, :]], axis=0)
    floats = lax.all_gather(floats, "dom", axis=1, tiled=True)
    integers = lax.all_gather(integers, "dom", axis=1, tiled=True)
    grid = (rows // LANES, LANES)
    all_blocks = floats[: coarse_slots * 9].reshape((coarse_slots, 3, 3) + grid)
    all_diagonal = floats[coarse_slots * 9 :].reshape((3,) + grid)
    all_columns = integers[:coarse_slots].reshape((coarse_slots,) + grid)
    permutation = integers[coarse_slots]
    ids = jnp.arange(rows, dtype=jnp.int32)
    inverse = jnp.sum(jnp.where(permutation[:, None] == ids[None, :], ids[:, None], 0), axis=0).reshape(grid)
    own_rows = jnp.pad(coarse_row_of_aggregate, (0, LANES - own)).reshape(1, LANES)

    def fine(field, smooth):
        before = lax.ppermute(field[:, chunks - margin :], "dom", up)
        after = lax.ppermute(field[:, :margin], "dom", down)
        padded = jnp.concatenate([before, field, after], axis=1)
        return pl.pallas_call(
            functools.partial(fine_kernel, smooth),
            out_shape=jax.ShapeDtypeStruct((3, chunks, LANES), jnp.float32),
        )(padded, index, blocks, diagonal, right)

    field = damping * right / diagonal
    for _ in range(SWEEPS - 1):
        field = fine(field, True)
    residual = fine(field, False)
    member = aggregate_of_node[None, :] == jnp.arange(own, dtype=jnp.int32)[:, None]
    flat = residual.reshape(3, nodes)
    sums = jnp.sum(jnp.where(member[None], flat[:, None, :], 0.0), axis=2)
    sums = lax.all_gather(sums, "dom", axis=1, tiled=True).reshape((3,) + grid)
    field, correction = pl.pallas_call(
        coarse_kernel,
        out_shape=(
            jax.ShapeDtypeStruct((3, chunks, LANES), jnp.float32),
            jax.ShapeDtypeStruct((3,) + grid, jnp.float32),
        ),
        scratch_shapes=[pltpu.VMEM((3,) + grid, jnp.float32), pltpu.VMEM((3,) + grid, jnp.float32)],
    )(sums, inverse, all_columns, all_blocks, all_diagonal, label, own_rows, field)
    correction = lax.dynamic_slice_in_dim(correction.reshape(3, rows), me * own, own, axis=1).T
    for _ in range(SWEEPS):
        field = fine(field, True)
    return (field.reshape(3, nodes).T, correction)


def solution(mesh):
    return jax.shard_map(
        per_device,
        mesh=mesh,
        in_specs=(
            P("dom", None),
            P("dom", None),
            P("dom", None),
            P("dom", None, None, None),
            P("dom"),
            P("dom"),
            P("dom", None),
            P("dom", None),
            P("dom", None, None, None),
        ),
        out_specs=(P("dom", None), P("dom", None)),
        check_vma=False,
    )
```

profile of v0, /device:TPU:103, one launch (start us, length us, event | category | flops | bytes accessed | tf_op | source)
XLA Modules:
  0.0 284.3 jit_solution(4648121122601075250)
XLA Ops:
  9.9 1.3 multiply_divide_fusion
  11.2 2.3 collective-permute-start
  13.6 2.2 collective-permute-start.1
  18.3 39.1 %all_gather.10 = s32[28,4096]{0,1:T(8,128)S(1)} all-gather(s32[28,32]{0,1:T(8,128)S(1)} %pad_add_fusion), channel_id=1, replica_groups=mesh['dom'=128] {'dom'}, dimensions={1}, use_global_device_ids=true | all-gather | bytes 462336 | tf_op jit(solution)/shard_map/all_gather | solution.py:131
  57.4 1.2 slice_reduce_fusion
  59.3 12.0 %select_reduce_fusion = s32[4096]{0:T(1024)} fusion(s32[4096]{0:T(1024)S(1)} %slice_reduce_fusion), kind=kLoop, calls=%fused_computation | loop fusion | flops 50327552 | bytes 32768 | tf_op jit(solution)/shard_map/reduce_sum | solution.py:138
  71.3 1.4 reshape.76
  74.5 2.5 shard_map.104.field_ref
  77.7 4.2 %collective-permute-start.2 = (f32[3,2,128]{2,1,0:T(2,128)S(1)}, f32[3,2,128]{2,1,0:T(2,128)S(1)}, u32[]{:S(2)}, u32[]{:S(2)}) collective-permute-start(f32[3,2,128]{2,1,0:T(2,128)S(1)} %get-tuple-element.13), channel_id=1, source_target_pairs={{0,1},{1,2},{2,3},{3,4},{4,5},{5,6},{6,7},{7,8},{8,9},{9,10},{10,1... | collective-permute-start | bytes 9224 | tf_op jit(solution)/shard_map/ppermute | solution.py:142
  81.9 1.9 collective-permute-start.3
  84.4 1.4 copy.46.column_ref
  85.8 5.2 %collective-permute-done.3 = f32[3,2,128]{2,1,0:T(2,128)S(1)} collective-permute-done((f32[3,2,128]{2,1,0:T(2,128)S(1)}, f32[3,2,128]{2,1,0:T(2,128)S(1)}, u32[]{:S(2)}, u32[]{:S(2)}) %collective-permute-start.3) | collective-permute-done | bytes 3104 | tf_op jit(solution)/shard_map/ppermute | solution.py:143
  91.0 1.3 pad_maximum_fusion.2.pad_ref
  92.4 2.5 shard_map.105
  95.7 31.6 %all-gather = f32[128,32,3]{1,2,0:T(4,128)S(1)} all-gather(f32[1,32,3]{1,2,0:T(4,128)S(1)} %bitcast.84), channel_id=1, replica_groups=mesh['dom'=128] {'dom'}, dimensions={0}, use_global_device_ids=true | all-gather | bytes 49536 | tf_op jit(solution)/shard_map/all_gather | solution.py:157
  128.1 2.2 slice.55
  130.3 1.2 copy.47.diagonal_ref
  131.5 5.6 %copy.42 = f32[243,4096]{1,0:T(8,128)} copy(f32[243,4096]{0,1:T(8,128)} %bitcast.64) | data formatting | bytes 7962624 | tf_op jit(solution)/shard_map/slice | solution.py:133
  137.1 2.9 %copy.53 = f32[31,8,32,128]{3,2,1,0:T(8,128)S(1)} copy(f32[31,8,32,128]{3,1,2,0:T(8,128)} %bitcast.61) | data formatting | bytes 8126464
  140.0 2.3 slice.59
  142.3 99.0 %shard_map.106 = (f32[3,8,128]{2,1,0:T(8,128)}, f32[3,32,128]{2,1,0:T(8,128)}) custom-call(f32[3,32,128]{2,1,0:T(8,128)} %bitcast.70, s32[32,128]{1,0:T(8,128)} %bitcast.78, s32[27,32,128]{2,1,0:T(8,128)} %copy.46.column_ref, f32[27,3,3,32,128]{4,3,2,1,0:T(8,128)} %bitcast.63, f32[3,32,128]{2,1,0:T(8,128)} %copy.47.diagonal_ref, s32[8,128]{1,0:T(8,128)} %bitcast.79, ...), custom_call_target="tpu_custom_call" | custom-call | tf_op jit(solution)/shard_map/pallas_call | solution.py:158
  242.0 5.5 %collective-permute-start.4 = (f32[3,2,128]{2,1,0:T(2,128)S(1)}, f32[3,2,128]{2,1,0:T(2,128)S(1)}, u32[]{:S(2)}, u32[]{:S(2)}) collective-permute-start(f32[3,2,128]{2,1,0:T(2,128)S(1)} %get-tuple-element.11), channel_id=1, source_target_pairs={{0,1},{1,2},{2,3},{3,4},{4,5},{5,6},{6,7},{7,8},{8,9},{9,10},{10,1... | collective-permute-start | bytes 9224 | tf_op jit(solution)/shard_map/ppermute | solution.py:142
  247.5 1.9 collective-permute-start.5
  250.3 6.4 %collective-permute-done.5 = f32[3,2,128]{2,1,0:T(2,128)S(1)} collective-permute-done((f32[3,2,128]{2,1,0:T(2,128)S(1)}, f32[3,2,128]{2,1,0:T(2,128)S(1)}, u32[]{:S(2)}, u32[]{:S(2)}) %collective-permute-start.5) | collective-permute-done | bytes 3104 | tf_op jit(solution)/shard_map/ppermute | solution.py:143
  256.7 1.3 pad_maximum_fusion.3.pad_ref
  258.0 2.5 shard_map.107
  261.3 1.9 collective-permute-start.6
  263.2 2.4 collective-permute-start.7
  266.2 6.1 %collective-permute-done.7 = f32[3,2,128]{2,1,0:T(2,128)S(1)} collective-permute-done((f32[3,2,128]{2,1,0:T(2,128)S(1)}, f32[3,2,128]{2,1,0:T(2,128)S(1)}, u32[]{:S(2)}, u32[]{:S(2)}) %collective-permute-start.7) | collective-permute-done | bytes 3104 | tf_op jit(solution)/shard_map/ppermute | solution.py:143
  272.3 1.3 pad_maximum_fusion.4.pad_ref
  273.6 2.5 shard_map.108
  276.1 1.3 copy.66
  (38 shorter events, 13.6 us)
Async XLA Ops:
  7.2 64.1 %copy-start = (s32[1024]{0:T(1024)S(1)}, s32[1024]{0:T(1024)}, u32[]{:S(2)}) copy-start(s32[1024]{0:T(1024)} %param.13) | copy-start | bytes 12292
  7.2 120.9 %all-gather.3.cloned.1.call-start = ((), (), s32[]{:S(2)}) async-start(), calls=%async_computation | async-start | bytes 4227072 | tf_op jit(solution)/shard_map/all_gather | solution.py:130
  11.2 62.6 %collective-permute-start = (f32[3,2,128]{2,1,0:T(2,128)S(1)}, f32[3,2,128]{2,1,0:T(2,128)S(1)}, u32[]{:S(2)}, u32[]{:S(2)}) collective-permute-start(f32[3,2,128]{2,1,0:T(2,128)S(1)} %get-tuple-element.15), channel_id=1, source_target_pairs={{0,1},{1,2},{2,3},{3,4},{4,5},{5,6},{6,7},{7,8},{8,9},{9,10},{10,1... | collective-permute-start | bytes 9224 | tf_op jit(solution)/shard_map/ppermute | solution.py:142
  13.6 60.3 %collective-permute-start.1 = (f32[3,2,128]{2,1,0:T(2,128)S(1)}, f32[3,2,128]{2,1,0:T(2,128)S(1)}, u32[]{:S(2)}, u32[]{:S(2)}) collective-permute-start(f32[3,2,128]{2,1,0:T(2,128)S(1)} %get-tuple-element.16), channel_id=1, source_target_pairs={{1,0},{2,1},{3,2},{4,3},{5,4},{6,5},{7,6},{8,7},{9,8},{10,9},{11,1... | collective-permute-start | bytes 9224 | tf_op jit(solution)/shard_map/ppermute | solution.py:143
  57.3 26.5 %copy-start.1 = (s32[32]{0:T(128)S(1)}, s32[32]{0:T(128)}, u32[]{:S(2)}) copy-start(s32[32]{0:T(128)} %param.14) | copy-start | bytes 388
  77.7 8.1 %collective-permute-start.2 = (f32[3,2,128]{2,1,0:T(2,128)S(1)}, f32[3,2,128]{2,1,0:T(2,128)S(1)}, u32[]{:S(2)}, u32[]{:S(2)}) collective-permute-start(f32[3,2,128]{2,1,0:T(2,128)S(1)} %get-tuple-element.13), channel_id=1, source_target_pairs={{0,1},{1,2},{2,3},{3,4},{4,5},{5,6},{6,7},{7,8},{8,9},{9,10},{10,1... | collective-permute-start | bytes 9224 | tf_op jit(solution)/shard_map/ppermute | solution.py:142
  81.9 9.1 %collective-permute-start.3 = (f32[3,2,128]{2,1,0:T(2,128)S(1)}, f32[3,2,128]{2,1,0:T(2,128)S(1)}, u32[]{:S(2)}, u32[]{:S(2)}) collective-permute-start(f32[3,2,128]{2,1,0:T(2,128)S(1)} %get-tuple-element.14), channel_id=1, source_target_pairs={{1,0},{2,1},{3,2},{4,3},{5,4},{6,5},{7,6},{8,7},{9,8},{10,9},{11,1... | collective-permute-start | bytes 9224 | tf_op jit(solution)/shard_map/ppermute | solution.py:143
  242.0 8.2 %collective-permute-start.4 = (f32[3,2,128]{2,1,0:T(2,128)S(1)}, f32[3,2,128]{2,1,0:T(2,128)S(1)}, u32[]{:S(2)}, u32[]{:S(2)}) collective-permute-start(f32[3,2,128]{2,1,0:T(2,128)S(1)} %get-tuple-element.11), channel_id=1, source_target_pairs={{0,1},{1,2},{2,3},{3,4},{4,5},{5,6},{6,7},{7,8},{8,9},{9,10},{10,1... | collective-permute-start | bytes 9224 | tf_op jit(solution)/shard_map/ppermute | solution.py:142
  247.5 9.1 %collective-permute-start.5 = (f32[3,2,128]{2,1,0:T(2,128)S(1)}, f32[3,2,128]{2,1,0:T(2,128)S(1)}, u32[]{:S(2)}, u32[]{:S(2)}) collective-permute-start(f32[3,2,128]{2,1,0:T(2,128)S(1)} %get-tuple-element.12), channel_id=1, source_target_pairs={{1,0},{2,1},{3,2},{4,3},{5,4},{6,5},{7,6},{8,7},{9,8},{10,9},{11,1... | collective-permute-start | bytes 9224 | tf_op jit(solution)/shard_map/ppermute | solution.py:143
  261.3 5.0 %collective-permute-start.6 = (f32[3,2,128]{2,1,0:T(2,128)S(1)}, f32[3,2,128]{2,1,0:T(2,128)S(1)}, u32[]{:S(2)}, u32[]{:S(2)}) collective-permute-start(f32[3,2,128]{2,1,0:T(2,128)S(1)} %get-tuple-element.9), channel_id=1, source_target_pairs={{0,1},{1,2},{2,3},{3,4},{4,5},{5,6},{6,7},{7,8},{8,9},{9,10},{10,1... | collective-permute-start | bytes 9224 | tf_op jit(solution)/shard_map/ppermute | solution.py:142
  263.2 9.1 %collective-permute-start.7 = (f32[3,2,128]{2,1,0:T(2,128)S(1)}, f32[3,2,128]{2,1,0:T(2,128)S(1)}, u32[]{:S(2)}, u32[]{:S(2)}) collective-permute-start(f32[3,2,128]{2,1,0:T(2,128)S(1)} %get-tuple-element.10), channel_id=1, source_target_pairs={{1,0},{2,1},{3,2},{4,3},{5,4},{6,5},{7,6},{8,7},{9,8},{10,9},{11,1... | collective-permute-start | bytes 9224 | tf_op jit(solution)/shard_map/ppermute | solution.py:143
Sparse Core Ops, SparseCore 0:
  11.1 65.9 all-gather.2
where the time goes:
time: 286 us; the launch traced here: 284 us
  Pallas kernels  109 us (38%)
  blocking collectives  70.7 us (25%)
  local copies, waits for them, and re-layouts  29.3 us (10%)
  starting transfers between devices  22.3 us (8%)
  other arithmetic  21.2 us (7%)
  waiting for transfers between devices  17.7 us (6%)
  between operations  14.2 us (5%)
    pallas_call x1, Pallas kernels, per_device(): pl.pallas_call(coarse_kernel, out_shape=(jax.ShapeDtypeStruct((3, chunks,...  99 us
    all_gather x1, blocking collectives, per_device(): integers = lax.all_gather(integers, 'dom', axis=1, tiled=True)  39.1 us
    all_gather x1, blocking collectives, per_device(): sums = lax.all_gather(sums, 'dom', axis=1, tiled=True).reshape((3,) + grid)  31.6 us
    ppermute x4, waiting for transfers between devices, fine(): after = lax.ppermute(field[:, :margin], 'dom', down)  17.7 us
    ppermute x4, starting transfers between devices, fine(): before = lax.ppermute(field[:, chunks - margin:], 'dom', up)  13.9 us
    reduce_sum x1, other arithmetic, per_device(): jnp.sum(jnp.where(permutation[:, None] == ids[None, :], ids[:, None], 0),...  12 us
    pallas_call x4, Pallas kernels, fine(): pl.pallas_call(functools.partial(fine_kernel, smooth), out_shape=jax.Shap...  9.99 us
    unnamed x13, local copies, waits for them, and re-layouts  9.57 us
  transfers between devices with their start and end apart: 9, of which 3 were waited for; matrix products, arithmetic and copies ran while one was open for 10% of the time, Pallas kernels for 2%

commit v1 on v0

v1 whole, which is shorter than its diff:
```python
import jax
import jax.numpy as jnp
from jax import lax
from jax.experimental import pallas as pl
from jax.experimental.pallas import tpu as pltpu
from jax.sharding import PartitionSpec as P

MESH = pl.DeviceIdType.MESH
LANES = 128
WIN = 256
CSWEEPS = 6
NEAR_BITS = (1, 2, 8, 32)
FAR_BITS = (4, 16, 64)
damping = 0.7


def subsets(bits):
    masks = [0]
    for bit in bits:
        masks = masks + [mask ^ bit for mask in masks]
    return sorted(masks[1:], key=lambda mask: -bin(mask).count("1"))


NEAR = subsets(NEAR_BITS)
FAR = subsets(FAR_BITS)
MEMBERS, BLOCKS = len(NEAR) + 1, len(FAR) + 1


def bit(value, position):
    return (value >> position) & 1


def member_of(device):
    return (device & 3) | (bit(device, 3) << 2) | (bit(device, 5) << 3)


def block_of(device):
    return bit(device, 2) | (bit(device, 4) << 1) | (bit(device, 6) << 2)


def place_of(row):
    device = row >> 5
    return (member_of(device) << 8) | (block_of(device) << 5) | (row & 31)


def pick(source, lane):
    return jnp.take_along_axis(source, lane, axis=1, mode="promise_in_bounds")


def spread(row, shape=(8, LANES)):
    return jnp.broadcast_to(row, shape)


def iota(shape, axis):
    return lax.broadcasted_iota(jnp.int32, shape, axis)


def kernel(
    right_ref, diagonal_ref, column_ref, block_ref, label_ref, own_ref, cdiagonal_ref, ccolumn_ref, cblock_ref,
    out_ref, correction_ref,
    right, diagonal, place, field, pulled, halo_out, halo_in, halo_new, node_place,
    before, aside, far_table, far_sums, near_table, coarse_block, coarse_place, inverse_chunk, inverse_lane, rhs, tile,
    halo_send, halo_recv, far_send, far_recv, near_send, near_recv,
):
    me = lax.axis_index("dom")
    devices = lax.axis_size("dom")
    member, block = member_of(me), block_of(me)
    after_me, before_me = lax.rem(me + 1, devices), lax.rem(me + devices - 1, devices)
    zero = jnp.zeros((8, LANES), jnp.float32)
    sub, lanes = iota((8, LANES), 0), iota((8, LANES), 1)

    barrier = pltpu.get_barrier_semaphore()
    for mask in FAR + NEAR:
        pl.semaphore_signal(barrier, inc=1, device_id=(me ^ mask,), device_id_type=MESH)
    for neighbour in (after_me, before_me):
        pl.semaphore_signal(barrier, inc=1, device_id=(neighbour,), device_id_type=MESH)

    def remote(source, target, send, recv, device):
        return pltpu.make_async_remote_copy(
            src_ref=source, dst_ref=target, send_sem=send, recv_sem=recv, device_id=(device,), device_id_type=MESH
        )

    def halo_copies(step):
        return [
            remote(halo_out.at[step, 0], halo_in.at[step, 0], halo_send.at[step, 0], halo_recv.at[step, 0], after_me),
            remote(halo_out.at[step, 1], halo_in.at[step, 1], halo_send.at[step, 1], halo_recv.at[step, 1], before_me),
        ]

    def send_halo(step, values):
        for c in range(3):
            halo_out[step, 0, 2 * c : 2 * c + 2, :] = values[c][6:8]
            halo_out[step, 1, 2 * c : 2 * c + 2, :] = values[c][0:2]
        if step == 0:
            halo_out[step, 0, 6:8, :] = node_place[6:8, :]
            halo_out[step, 1, 6:8, :] = node_place[0:2, :]
        else:
            halo_out[step, 0, 6:8, :] = zero[0:2]
            halo_out[step, 1, 6:8, :] = zero[0:2]
        for copy in halo_copies(step):
            copy.start()

    def wait_halo(step):
        for copy in halo_copies(step):
            copy.wait_recv()

    def send_near(step):
        own = near_table.at[step, member]
        for mask in NEAR:
            remote(own, own, near_send.at[step], near_recv.at[step], me ^ mask).start()

    def wait_near(step, sems):
        whole = near_table.at[step, pl.ds(0, MEMBERS - 1)]
        pltpu.make_async_copy(whole, whole, sems.at[step]).wait()

    def send_far(own, index):
        for mask in FAR:
            remote(own, own, far_send.at[index], far_recv.at[index], me ^ mask).start()

    def wait_far(table, index, sems):
        whole = table.at[pl.ds(0, BLOCKS - 1)]
        pltpu.make_async_copy(whole, whole, sems.at[index]).wait()

    for c in range(3):
        for j in range(8):
            span = slice(j * LANES, (j + 1) * LANES)
            right[c, j : j + 1, :] = right_ref[c : c + 1, span]
            diagonal[c, j : j + 1, :] = diagonal_ref[c : c + 1, span]
    own_place = place_of(own_ref[...])
    aside[...] = jnp.zeros((16, LANES), jnp.float32)
    aside[8:9, 0:32] = own_place.astype(jnp.float32)
    node_place[...] = pick(spread(aside[8:9, :]), label_ref[...])
    state = [damping * right[c] / diagonal[c] for c in range(3)]
    for c in range(3):
        field[c] = state[c]

    pl.semaphore_wait(barrier, len(FAR) + len(NEAR) + 2)
    send_halo(0, state)

    before[...] = jnp.zeros(before.shape, jnp.float32)
    for i in range(3):
        for c in range(3):
            q = 3 * i + c
            before[32 * q : 32 * q + 32, 0:27] = cblock_ref[i, c]
    before[288:320, 0:27] = place_of(ccolumn_ref[...]).astype(jnp.float32)
    aside[0:3, 0:32] = cdiagonal_ref[...]
    own_block = far_table.at[block]
    for group in range(3):
        turned = before[128 * group : 128 * group + 128, :].T
        own_block[32 * group : 32 * group + 32, :] = turned[0:32, :]
    extra = pltpu.roll(aside[0:8, :], 64, 1) + pltpu.roll(aside[8:16, :], 96, 1)
    own_block[64:72, :] = own_block[64:72, :] + extra
    send_far(own_block, 0)

    place[24:32, :] = jnp.zeros((8, 8 * LANES), jnp.int32)
    for j in range(8):
        span = slice(j * LANES, (j + 1) * LANES)
        start = me * (8 * LANES) + (j * LANES - WIN)
        for k in range(4):
            rows = slice(8 * k, min(8 * k + 8, 27))
            place[rows, span] = column_ref[rows, span] - start

    def apply_fine(low, high):
        for j in range(8):
            span = slice(j * LANES, (j + 1) * LANES)
            source = []
            for c in range(3):
                line = []
                for t in range(5):
                    at = j + t
                    if at < 2:
                        line.append(low[2 * c + at : 2 * c + at + 1, :])
                    elif at < 10:
                        line.append(field[c, at - 2 : at - 1, :])
                    else:
                        line.append(high[2 * c + at - 10 : 2 * c + at - 9, :])
                source.append(line)
            total = [None] * 3
            tail = [None] * 3
            for k in range(4):
                where = place[8 * k : 8 * k + 8, span]
                lane, chunk = where & (LANES - 1), where >> 7
                masks = [chunk == t for t in range(1, 5)]
                for c in range(3):
                    near = pick(spread(source[c][0]), lane)
                    for t in range(1, 5):
                        near = jnp.where(masks[t - 1], pick(spread(source[c][t]), lane), near)
                    for i in range(3):
                        if k < 3:
                            term = block_ref[i, c, 8 * k : 8 * k + 8, span] * near
                            total[i] = term if total[i] is None else total[i] + term
                        else:
                            term = block_ref[i, c, 24:27, span] * near[0:3]
                            tail[i] = term if tail[i] is None else tail[i] + term
            for i in range(3):
                pulled[i, j : j + 1, :] = jnp.sum(total[i], axis=0, keepdims=True) + jnp.sum(
                    tail[i], axis=0, keepdims=True
                )
        return [right[i] - (diagonal[i] * field[i] - pulled[i]) for i in range(3)]

    def smooth(low, high):
        residual = apply_fine(low, high)
        values = [field[i] + damping * residual[i] / diagonal[i] for i in range(3)]
        for i in range(3):
            field[i] = values[i]
        return values

    wait_halo(0)
    send_halo(1, smooth(halo_in.at[0, 0], halo_in.at[0, 1]))
    wait_halo(1)
    residual = apply_fine(halo_in.at[1, 0], halo_in.at[1, 1])

    sums = [[zero] * 4 for _ in range(3)]
    for j in range(8):
        label = spread(label_ref[j : j + 1, :])
        for a in range(4):
            mine = label == sub + 8 * a
            for c in range(3):
                sums[c][a] = sums[c][a] + jnp.where(mine, spread(residual[c][j : j + 1, :]), 0.0)
    stacked = jnp.concatenate([part for line in sums for part in line] + [zero] * 4, axis=0)
    far_sums[block] = jnp.sum(stacked.T, axis=0, keepdims=True)
    send_far(far_sums.at[block], 1)

    wait_far(far_table, 0, far_recv)
    part = lanes >> 5
    for h in range(2):
        for k in range(4):
            rows = 32 * h + 8 * k
            for group in range(3):
                come = [far_table[4 * h + jj, 32 * group + 8 * k : 32 * group + 8 * k + 8, :] for jj in range(4)]
                for quarter in range(4):
                    q = 4 * group + quarter
                    if q > 9 and k > 0:
                        continue
                    value = None
                    for jj in range(4):
                        shift = (32 * (jj - quarter)) % LANES
                        moved = pltpu.roll(come[jj], shift, 1) if shift else come[jj]
                        value = moved if value is None else jnp.where(part == jj, moved, value)
                    if q < 9:
                        coarse_block[q, rows : rows + 8, :] = value
                    elif q == 9:
                        coarse_place[rows : rows + 8, :] = value.astype(jnp.int32)
                    elif q == 10:
                        tile[3 * h : 3 * h + 3, :] = value[0:3]
                    else:
                        tile[6 + h : 7 + h, :] = value[0:1]
    near_table[0, member] = tile[...]
    send_near(0)

    wait_far(far_sums, 1, far_recv)
    gathered = zero
    component = jnp.where(sub < 3, sub, sub - 3)
    lane = (jnp.where(sub < 6, component, 0) << 5) | (lanes & 31)
    for j in range(BLOCKS):
        mine = (part == j % 4) & (sub >= 3 * (j // 4)) & (sub < 3 * (j // 4) + 3)
        gathered = jnp.where(mine, pick(spread(far_sums[j]), lane), gathered)
    near_table[1, member] = gathered
    send_near(1)

    wait_near(0, near_recv)
    found = jnp.zeros((64, LANES), jnp.float32)
    high_id, low_id = iota((32, LANES), 0), iota((LANES, LANES), 0)
    lane_id = iota((32, LANES), 1)
    for m in range(MEMBERS):
        left, turn = [], []
        for h in range(2):
            where = near_table[0, m, 6 + h : 7 + h, :].astype(jnp.int32)
            hit = spread(where >> 7, (32, LANES)) == high_id
            left.append(
                jnp.concatenate(
                    [
                        jnp.where(hit, jnp.float32(2 * m + h), 0.0),
                        jnp.where(hit, lane_id.astype(jnp.float32), 0.0),
                    ],
                    axis=0,
                )
            )
            turn.append(jnp.where(spread(where & (LANES - 1), (LANES, LANES)) == low_id, 1.0, 0.0))
        found = found + lax.dot_general(
            jnp.concatenate(left, axis=1).astype(jnp.bfloat16),
            jnp.concatenate(turn, axis=1).astype(jnp.bfloat16),
            (((1,), (1,)), ((), ())),
            preferred_element_type=jnp.float32,
        )
    inverse_chunk[...] = found[0:32].astype(jnp.int32)
    inverse_lane[...] = found[32:64].astype(jnp.int32)

    wait_near(1, near_recv)
    near_sums = [near_table[1, m] for m in range(MEMBERS)]
    for m in range(MEMBERS):
        halves = []
        for h in range(2):
            row = 2 * m + h
            chunk = spread(inverse_chunk[row : row + 1, :])
            lane = spread(inverse_lane[row : row + 1, :])
            owner = chunk >> 1
            value = zero
            for n in range(MEMBERS):
                value = jnp.where(owner == n, pick(near_sums[n], lane), value)
            first, second = (value, pltpu.roll(value, 5, 0)) if h == 0 else (pltpu.roll(value, 3, 0), value)
            halves.append(jnp.where((chunk & 1) == 0, first, second))
        value = jnp.where(sub < 3, halves[0], jnp.where(sub < 6, halves[1], 0.0))
        rhs[m] = value
        near_table[2, m] = damping * value / jnp.where(sub < 6, near_table[0, m], 1.0)

    own_diagonal = jnp.where(sub < 6, near_table[0, member], 1.0)

    def source_row(step, chunk, c):
        at = 3 * (chunk % 2) + c
        return near_table[step, chunk // 2, at : at + 1, :]

    def coarse_sweep(step):
        for h in range(2):
            total = [zero] * 3
            for k in range(4):
                rows = 32 * h + 8 * k
                where = coarse_place[rows : rows + 8, :]
                lane, chunk = where & (LANES - 1), where >> 7
                near = [zero] * 3
                for n in range(2 * MEMBERS):
                    mine = chunk == n
                    for c in range(3):
                        near[c] = jnp.where(mine, pick(spread(source_row(step, n, c)), lane), near[c])
                for i in range(3):
                    for c in range(3):
                        total[i] = total[i] + coarse_block[3 * i + c, rows : rows + 8, :] * near[c]
            for i in range(3):
                tile[3 * h + i : 3 * h + i + 1, :] = jnp.sum(total[i], axis=0, keepdims=True)
        old = near_table[step, member]
        pull = jnp.where(sub < 6, tile[...], 0.0)
        return old + damping * (rhs[member] - (own_diagonal * old - pull)) / own_diagonal

    def sweep(step, carry):
        near_table[step + 1, member] = coarse_sweep(step)
        send_near(step + 1)
        wait_near(step + 1, near_recv)
        return carry

    lax.fori_loop(2, 2 + CSWEEPS - 1, sweep, 0)
    last = 1 + CSWEEPS

    mine = near_table[last, member]
    mine = jnp.where(block >= 4, pltpu.roll(mine, 5, 0), mine)
    quarter = block & 3
    shown = mine
    for jj in range(1, 4):
        shown = jnp.where(quarter == jj, pltpu.roll(mine, LANES - 32 * jj, 1), shown)
    correction_ref[...] = shown[0:3, 0:32]

    halo_place = [halo_in[0, 0, 6:8, :], halo_in[0, 1, 6:8, :]]
    where_own = node_place[...].astype(jnp.int32)
    halo_new[0, 0:2, :] = halo_place[0]
    halo_new[0, 2:4, :] = halo_place[1]
    halo_new[0, 4:8, :] = zero[0:4]
    where_halo = halo_new[0].astype(jnp.int32)
    lane_own, chunk_own = where_own & (LANES - 1), where_own >> 7
    lane_halo, chunk_halo = where_halo & (LANES - 1), where_halo >> 7
    add_own, add_halo = [zero] * 3, [zero] * 3
    for n in range(2 * MEMBERS):
        for c in range(3):
            source = spread(source_row(last, n, c))
            add_own[c] = jnp.where(chunk_own == n, pick(source, lane_own), add_own[c])
            add_halo[c] = jnp.where(chunk_halo == n, pick(source, lane_halo), add_halo[c])
    for c in range(3):
        field[c] = field[c] + add_own[c]
        halo_new[0, 2 * c : 2 * c + 2, :] = halo_in[1, 0, 2 * c : 2 * c + 2, :] + add_halo[c][0:2]
        halo_new[1, 2 * c : 2 * c + 2, :] = halo_in[1, 1, 2 * c : 2 * c + 2, :] + add_halo[c][2:4]

    send_halo(2, smooth(halo_new.at[0], halo_new.at[1]))
    wait_halo(2)
    values = smooth(halo_in.at[2, 0], halo_in.at[2, 1])
    for c in range(3):
        for j in range(8):
            out_ref[c : c + 1, j * LANES : (j + 1) * LANES] = values[c][j : j + 1]

    for step in range(3):
        for copy in halo_copies(step):
            copy.wait_send()
    wait_far(far_table, 0, far_send)
    wait_far(far_sums, 1, far_send)
    for step in range(2):
        wait_near(step, near_send)

    def drain(step, carry):
        wait_near(step, near_send)
        return carry

    lax.fori_loop(3, 2 + CSWEEPS, drain, 0)


def per_device(
    right_side,
    fine_diagonal,
    fine_columns,
    fine_blocks,
    aggregate_of_node,
    coarse_row_of_aggregate,
    coarse_diagonal,
    coarse_columns,
    coarse_blocks,
):
    nodes = right_side.shape[0]
    own = coarse_diagonal.shape[0]
    steps = 2 + CSWEEPS
    f32 = jnp.float32
    vmem = pl.BlockSpec(memory_space=pltpu.VMEM)
    field, correction = pl.pallas_call(
        kernel,
        out_shape=(jax.ShapeDtypeStruct((3, nodes), f32), jax.ShapeDtypeStruct((3, own), f32)),
        in_specs=[vmem] * 9,
        out_specs=(vmem, vmem),
        scratch_shapes=[
            pltpu.VMEM((3, 8, LANES), f32),
            pltpu.VMEM((3, 8, LANES), f32),
            pltpu.VMEM((32, nodes), jnp.int32),
            pltpu.VMEM((3, 8, LANES), f32),
            pltpu.VMEM((3, 8, LANES), f32),
            pltpu.VMEM((3, 2, 8, LANES), f32),
            pltpu.VMEM((3, 2, 8, LANES), f32),
            pltpu.VMEM((2, 8, LANES), f32),
            pltpu.VMEM((8, LANES), f32),
            pltpu.VMEM((384, LANES), f32),
            pltpu.VMEM((16, LANES), f32),
            pltpu.VMEM((BLOCKS, 96, LANES), f32),
            pltpu.VMEM((BLOCKS, 1, LANES), f32),
            pltpu.VMEM((steps, MEMBERS, 8, LANES), f32),
            pltpu.VMEM((9, 64, LANES), f32),
            pltpu.VMEM((64, LANES), jnp.int32),
            pltpu.VMEM((32, LANES), jnp.int32),
            pltpu.VMEM((32, LANES), jnp.int32),
            pltpu.VMEM((MEMBERS, 8, LANES), f32),
            pltpu.VMEM((8, LANES), f32),
            pltpu.SemaphoreType.DMA((3, 2)),
            pltpu.SemaphoreType.DMA((3, 2)),
            pltpu.SemaphoreType.DMA((2,)),
            pltpu.SemaphoreType.DMA((2,)),
            pltpu.SemaphoreType.DMA((steps,)),
            pltpu.SemaphoreType.DMA((steps,)),
        ],
        compiler_params=pltpu.CompilerParams(collective_id=0, has_side_effects=True),
    )(
        right_side.T,
        fine_diagonal.T,
        fine_columns.T,
        jnp.transpose(fine_blocks, (2, 3, 1, 0)),
        aggregate_of_node.reshape(8, LANES),
        coarse_row_of_aggregate.reshape(1, own),
        coarse_diagonal.T,
        coarse_columns,
        jnp.transpose(coarse_blocks, (2, 3, 0, 1)),
    )
    return (field.T, correction.T)


def solution(mesh):
    return jax.shard_map(
        per_device,
        mesh=mesh,
        in_specs=(
            P("dom", None),
            P("dom", None),
            P("dom", None),
            P("dom", None, None, None),
            P("dom"),
            P("dom"),
            P("dom", None),
            P("dom", None),
            P("dom", None, None, None),
        ),
        out_specs=(P("dom", None), P("dom", None)),
        check_vma=False,
    )
```

time: 286 us -> 67.4 us (0.24)
  the two profiles are of different devices: /device:TPU:103 before, /device:TPU:0 now
where the time goes in v1:
time: 67.4 us; the launch traced here: 67.2 us
  Pallas kernels  64 us (95%)
  local copies, waits for them, and re-layouts  2.56 us (4%)
    pallas_call x1, Pallas kernels, per_device(): pl.pallas_call(kernel, out_shape=(jax.ShapeDtypeStruct((3, nodes), f32),...  64 us
    unnamed x2, local copies, waits for them, and re-layouts  2.56 us

profile of v1, /device:TPU:0, one launch (start us, length us, event | category | flops | bytes accessed | tf_op | source)
XLA Modules:
  0.0 67.2 jit_solution(3666224684467193096)
XLA Ops:
  0.6 64.0 %shard_map.104 = (f32[3,1024]{1,0:T(4,128)}, f32[3,32]{1,0:T(4,128)}) custom-call(f32[3,1024]{1,0:T(4,128)} %bitcast.13, f32[3,1024]{1,0:T(4,128)} %bitcast.14, s32[27,1024]{1,0:T(8,128)} %bitcast.12, f32[3,3,27,1024]{3,2,1,0:T(8,128)} %bitcast.10, s32[8,128]{1,0:T(8,128)} %bitcast.16, s32[1,32]{1,0:T(1,128)} %bitcast.19, f32[3,32]{1,0:T(4,128)} %bitcast.17, ...), custom_call_target="tpu_custom_call" | custom-call | tf_op jit(solution)/shard_map/pallas_call | solution.py:407
  64.6 1.3 %copy.13 = f32[1024,3]{0,1:T(4,128)} copy(f32[1024,3]{0,1:T(4,128)} %bitcast.15) | data formatting | bytes 24576
  66.0 1.2 %copy.14 = f32[32,3]{0,1:T(4,128)} copy(f32[32,3]{0,1:T(4,128)} %bitcast.18) | data formatting | bytes 768

commit v2 on v1

v2 whole, which is shorter than its diff:
```python
import jax
import jax.numpy as jnp
from jax import lax
from jax.experimental import pallas as pl
from jax.experimental.pallas import tpu as pltpu
from jax.sharding import PartitionSpec as P

MESH = pl.DeviceIdType.MESH
LANES = 128
WIN = 256
CSWEEPS = 6
NEAR_BITS = (1, 2, 8, 32)
FAR_BITS = (4, 16, 64)
damping = 0.7


def subsets(bits):
    masks = [0]
    for bit in bits:
        masks = masks + [mask ^ bit for mask in masks]
    return sorted(masks[1:], key=lambda mask: -bin(mask).count("1"))


NEAR = subsets(NEAR_BITS)
FAR = subsets(FAR_BITS)
MEMBERS, BLOCKS = len(NEAR) + 1, len(FAR) + 1


def bit(value, position):
    return (value >> position) & 1


def member_of(device):
    return (device & 3) | (bit(device, 3) << 2) | (bit(device, 5) << 3)


def block_of(device):
    return bit(device, 2) | (bit(device, 4) << 1) | (bit(device, 6) << 2)


def place_of(row):
    device = row >> 5
    return (member_of(device) << 8) | (block_of(device) << 5) | (row & 31)


def pick(source, lane):
    return jnp.take_along_axis(source, lane, axis=1, mode="promise_in_bounds")


def spread(row, shape=(8, LANES)):
    return jnp.broadcast_to(row, shape)


def iota(shape, axis):
    return lax.broadcasted_iota(jnp.int32, shape, axis)


def kernel(
    right_hbm, diagonal_hbm, column_hbm, block_hbm, label_hbm, own_hbm, cdiagonal_hbm, ccolumn_hbm, cblock_hbm,
    out_ref, correction_ref,
    right_ref, diagonal_ref, column_ref, block_ref, label_ref, own_ref, cdiagonal_ref, ccolumn_ref, cblock_ref,
    right, diagonal, place, first, second, third, fourth, pulled, halo_out, halo_in, node_place, edge_out, edge_in,
    halo_block, halo_column,
    before, aside, far_table, far_sums, near_table, coarse_block, coarse_place, inverse_chunk, inverse_lane, rhs, tile,
    load_sem, halo_send, halo_recv, far_send, far_recv, near_send, near_recv,
):
    me = lax.axis_index("dom")
    devices = lax.axis_size("dom")
    member, block = member_of(me), block_of(me)
    after_me, before_me = lax.rem(me + 1, devices), lax.rem(me + devices - 1, devices)
    has_after, has_before = me < devices - 1, me > 0
    zero = jnp.zeros((8, LANES), jnp.float32)
    sub, lanes = iota((8, LANES), 0), iota((8, LANES), 1)

    barrier = pltpu.get_barrier_semaphore()

    def greet(device):
        pl.semaphore_signal(barrier, inc=1, device_id=(device,), device_id_type=MESH)

    for mask in FAR + NEAR:
        greet(me ^ mask)
    pl.when(has_after)(lambda: greet(after_me))
    pl.when(has_before)(lambda: greet(before_me))

    loads = [
        pltpu.make_async_copy(source, target, load_sem.at[index])
        for index, (source, target) in enumerate(
            [
                (right_hbm, right_ref),
                (diagonal_hbm, diagonal_ref),
                (column_hbm, column_ref),
                (block_hbm, block_ref),
                (label_hbm, label_ref),
                (own_hbm, own_ref),
                (cdiagonal_hbm, cdiagonal_ref),
                (ccolumn_hbm, ccolumn_ref),
                (cblock_hbm, cblock_ref),
            ]
        )
    ]
    for index in (0, 1, 4, 5, 2, 3, 8, 7, 6):
        loads[index].start()

    def remote(source, target, send, recv, device):
        return pltpu.make_async_remote_copy(
            src_ref=source, dst_ref=target, send_sem=send, recv_sem=recv, device_id=(device,), device_id_type=MESH
        )

    def halo_pair(step):
        if step == 0:
            sources = [halo_out.at[0], halo_out.at[1]]
            targets = [halo_in.at[0], halo_in.at[1]]
        elif step == 1:
            sources = [block_ref.at[:, :, :, 768:1024], block_ref.at[:, :, :, 0:256]]
            targets = [halo_block.at[0], halo_block.at[1]]
        elif step == 2:
            sources = [column_ref.at[:, 768:1024], column_ref.at[:, 0:256]]
            targets = [halo_column.at[0], halo_column.at[1]]
        else:
            sources = [edge_out.at[0], edge_out.at[1]]
            targets = [edge_in.at[0], edge_in.at[1]]
        return [
            remote(sources[d], targets[d], halo_send.at[step, d], halo_recv.at[step, d], device)
            for d, device in enumerate((after_me, before_me))
        ]

    def send_halo(step):
        ahead, back = halo_pair(step)
        pl.when(has_after)(ahead.start)
        pl.when(has_before)(back.start)

    def wait_halo(step):
        ahead, back = halo_pair(step)
        pl.when(has_before)(ahead.wait_recv)
        pl.when(has_after)(back.wait_recv)

    def close_halo(step):
        ahead, back = halo_pair(step)
        pl.when(has_after)(ahead.wait_send)
        pl.when(has_before)(back.wait_send)

    def send_near(step):
        own = near_table.at[step, member]
        for mask in NEAR:
            remote(own, own, near_send.at[step], near_recv.at[step], me ^ mask).start()

    def wait_near(step, sems):
        whole = near_table.at[step, pl.ds(0, MEMBERS - 1)]
        pltpu.make_async_copy(whole, whole, sems.at[step]).wait()

    def send_far(own, index):
        for mask in FAR:
            remote(own, own, far_send.at[index], far_recv.at[index], me ^ mask).start()

    def wait_far(table, index, sems):
        whole = table.at[pl.ds(0, BLOCKS - 1)]
        pltpu.make_async_copy(whole, whole, sems.at[index]).wait()

    def apply_fine(field, chunks):
        for j in chunks:
            if j < 0:
                matrix, span = halo_block.at[0], slice((j + 2) * LANES, (j + 3) * LANES)
            elif j < 8:
                matrix, span = block_ref, slice(j * LANES, (j + 1) * LANES)
            else:
                matrix, span = halo_block.at[1], slice((j - 8) * LANES, (j - 7) * LANES)
            here = slice((j + 2) * LANES, (j + 3) * LANES)
            source = [[field[c, j + t + 2 : j + t + 3, :] for t in range(5)] for c in range(3)]
            total = [None] * 3
            tail = [None] * 3
            for k in range(4):
                where = place[8 * k : 8 * k + 8, here]
                lane, chunk = where & (LANES - 1), where >> 7
                masks = [chunk == t for t in range(1, 5)]
                for c in range(3):
                    near = pick(spread(source[c][0]), lane)
                    for t in range(1, 5):
                        near = jnp.where(masks[t - 1], pick(spread(source[c][t]), lane), near)
                    for i in range(3):
                        if k < 3:
                            term = matrix[i, c, 8 * k : 8 * k + 8, span] * near
                            total[i] = term if total[i] is None else total[i] + term
                        else:
                            term = matrix[i, c, 24:27, span] * near[0:3]
                            tail[i] = term if tail[i] is None else tail[i] + term
            for i in range(3):
                pulled[i, j + 4 : j + 5, :] = jnp.sum(total[i], axis=0, keepdims=True) + jnp.sum(
                    tail[i], axis=0, keepdims=True
                )

    def residual_of(field, c, low, high):
        rows = slice(low + 4, high + 4)
        return right[c, rows, :] - (diagonal[c, rows, :] * field[c, rows, :] - pulled[c, rows, :])

    def smooth(field, target, low, high):
        rows = slice(low + 4, high + 4)
        for c in range(3):
            target[c, rows, :] = field[c, rows, :] + damping * residual_of(field, c, low, high) / diagonal[c, rows, :]

    def place_columns(source, chunks, offset):
        for j in chunks:
            span = slice((j - offset) * LANES, (j - offset + 1) * LANES)
            here = slice((j + 2) * LANES, (j + 3) * LANES)
            start = me * (8 * LANES) + (j * LANES - WIN)
            for k in range(4):
                rows = slice(8 * k, min(8 * k + 8, 27))
                place[rows, here] = source[rows, span] - start

    place[24:32, :] = jnp.zeros((8, 12 * LANES), jnp.int32)
    before[...] = jnp.zeros(before.shape, jnp.float32)
    aside[...] = jnp.zeros(aside.shape, jnp.float32)
    for index in (0, 1, 4, 5):
        loads[index].wait()
    for c in range(3):
        for j in range(8):
            span = slice(j * LANES, (j + 1) * LANES)
            right[c, j + 4 : j + 5, :] = right_ref[c : c + 1, span]
            diagonal[c, j + 4 : j + 5, :] = diagonal_ref[c : c + 1, span]
    aside[8:9, 0:32] = place_of(own_ref[...]).astype(jnp.float32)
    node_place[...] = pick(spread(aside[8:9, :]), label_ref[...])
    for c in range(3):
        first[c, 4:12, :] = damping * right[c, 4:12, :] / diagonal[c, 4:12, :]
        for d in range(2):
            rows = slice(8, 12) if d == 0 else slice(4, 8)
            halo_out[d, 4 * c : 4 * c + 4, :] = right[c, rows, :]
            halo_out[d, 12 + 4 * c : 16 + 4 * c, :] = diagonal[c, rows, :]
    halo_out[0, 24:28, :] = node_place[4:8, :]
    halo_out[1, 24:28, :] = node_place[0:4, :]
    halo_out[0, 28:32, :] = zero[0:4]
    halo_out[1, 28:32, :] = zero[0:4]

    loads[2].wait()
    place_columns(column_ref, range(8), 0)
    loads[3].wait()
    apply_fine(first, range(2, 6))
    smooth(first, second, 2, 6)
    for c in range(3):
        edge_out[0, 2 * c : 2 * c + 2, :] = second[c, 8:10, :]
        edge_out[1, 2 * c : 2 * c + 2, :] = second[c, 6:8, :]
    edge_out[0, 6:8, :] = zero[0:2]
    edge_out[1, 6:8, :] = zero[0:2]

    for index in (6, 7, 8):
        loads[index].wait()
    for i in range(3):
        for c in range(3):
            q = 3 * i + c
            before[32 * q : 32 * q + 32, 0:27] = cblock_ref[i, c]
    before[288:320, 0:27] = place_of(ccolumn_ref[...]).astype(jnp.float32)
    aside[0:3, 0:32] = cdiagonal_ref[...]
    own_block = far_table.at[block]
    for group in range(3):
        turned = before[128 * group : 128 * group + 128, :].T
        own_block[32 * group : 32 * group + 32, :] = turned[0:32, :]
    extra = pltpu.roll(aside[0:8, :], 64, 1) + pltpu.roll(aside[8:16, :], 96, 1)
    own_block[64:72, :] = own_block[64:72, :] + extra

    neighbours = has_after.astype(jnp.int32) + has_before.astype(jnp.int32)
    pl.semaphore_wait(barrier, len(FAR) + len(NEAR) + neighbours)
    for step in range(4):
        send_halo(step)

    wait_halo(0)
    for c in range(3):
        for d, rows in enumerate((slice(0, 4), slice(12, 16))):
            right[c, rows, :] = halo_in[d, 4 * c : 4 * c + 4, :]
            diagonal[c, rows, :] = halo_in[d, 12 + 4 * c : 16 + 4 * c, :]
            first[c, rows, :] = damping * right[c, rows, :] / diagonal[c, rows, :]
    apply_fine(first, (0, 1, 6, 7))
    smooth(first, second, 0, 2)
    smooth(first, second, 6, 8)
    apply_fine(second, range(2, 6))

    def add_up(sums, chunks):
        for j in chunks:
            label = spread(label_ref[j : j + 1, :])
            lines = [residual_of(second, c, j, j + 1) for c in range(3)]
            for a in range(4):
                mine = label == sub + 8 * a
                for c in range(3):
                    sums[c][a] = sums[c][a] + jnp.where(mine, spread(lines[c]), 0.0)

    sums = [[zero] * 4 for _ in range(3)]
    add_up(sums, range(2, 6))

    wait_halo(1)
    wait_halo(2)
    place_columns(halo_column.at[0], (-2, -1), -2)
    place_columns(halo_column.at[1], (8, 9), 8)
    apply_fine(first, (-2, -1, 8, 9))
    smooth(first, second, -2, 0)
    smooth(first, second, 8, 10)
    apply_fine(second, (0, 1, 6, 7))
    add_up(sums, (0, 1, 6, 7))
    stacked = jnp.concatenate([part for line in sums for part in line] + [zero] * 4, axis=0)
    far_sums[block] = jnp.sum(stacked.T, axis=0, keepdims=True)
    send_far(far_sums.at[block], 1)
    send_far(own_block, 0)

    wait_far(far_table, 0, far_recv)
    part = lanes >> 5
    for h in range(2):
        for k in range(4):
            rows = 32 * h + 8 * k
            for group in range(3):
                come = [far_table[4 * h + jj, 32 * group + 8 * k : 32 * group + 8 * k + 8, :] for jj in range(4)]
                for quarter in range(4):
                    q = 4 * group + quarter
                    if q > 9 and k > 0:
                        continue
                    value = None
                    for jj in range(4):
                        shift = (32 * (jj - quarter)) % LANES
                        moved = pltpu.roll(come[jj], shift, 1) if shift else come[jj]
                        value = moved if value is None else jnp.where(part == jj, moved, value)
                    if q < 9:
                        coarse_block[q, rows : rows + 8, :] = value
                    elif q == 9:
                        coarse_place[rows : rows + 8, :] = value.astype(jnp.int32)
                    elif q == 10:
                        tile[3 * h : 3 * h + 3, :] = value[0:3]
                    else:
                        tile[6 + h : 7 + h, :] = value[0:1]
    near_table[0, member] = tile[...]
    send_near(0)

    wait_far(far_sums, 1, far_recv)
    gathered = zero
    component = jnp.where(sub < 3, sub, sub - 3)
    lane = (jnp.where(sub < 6, component, 0) << 5) | (lanes & 31)
    for j in range(BLOCKS):
        mine = (part == j % 4) & (sub >= 3 * (j // 4)) & (sub < 3 * (j // 4) + 3)
        gathered = jnp.where(mine, pick(spread(far_sums[j]), lane), gathered)
    near_table[1, member] = gathered
    send_near(1)

    wait_near(0, near_recv)
    found = jnp.zeros((64, LANES), jnp.float32)
    high_id, low_id = iota((32, LANES), 0), iota((LANES, LANES), 0)
    lane_id = iota((32, LANES), 1)
    for m in range(MEMBERS):
        left, turn = [], []
        for h in range(2):
            where = near_table[0, m, 6 + h : 7 + h, :].astype(jnp.int32)
            hit = spread(where >> 7, (32, LANES)) == high_id
            left.append(
                jnp.concatenate(
                    [
                        jnp.where(hit, jnp.float32(2 * m + h), 0.0),
                        jnp.where(hit, lane_id.astype(jnp.float32), 0.0),
                    ],
                    axis=0,
                )
            )
            turn.append(jnp.where(spread(where & (LANES - 1), (LANES, LANES)) == low_id, 1.0, 0.0))
        found = found + lax.dot_general(
            jnp.concatenate(left, axis=1).astype(jnp.bfloat16),
            jnp.concatenate(turn, axis=1).astype(jnp.bfloat16),
            (((1,), (1,)), ((), ())),
            preferred_element_type=jnp.float32,
        )
    inverse_chunk[...] = found[0:32].astype(jnp.int32)
    inverse_lane[...] = found[32:64].astype(jnp.int32)

    wait_near(1, near_recv)
    near_sums = [near_table[1, m] for m in range(MEMBERS)]
    for m in range(MEMBERS):
        halves = []
        for h in range(2):
            row = 2 * m + h
            chunk = spread(inverse_chunk[row : row + 1, :])
            lane = spread(inverse_lane[row : row + 1, :])
            owner = chunk >> 1
            value = zero
            for n in range(MEMBERS):
                value = jnp.where(owner == n, pick(near_sums[n], lane), value)
            low, high = (value, pltpu.roll(value, 5, 0)) if h == 0 else (pltpu.roll(value, 3, 0), value)
            halves.append(jnp.where((chunk & 1) == 0, low, high))
        value = jnp.where(sub < 3, halves[0], jnp.where(sub < 6, halves[1], 0.0))
        rhs[m] = value
        near_table[2, m] = damping * value / jnp.where(sub < 6, near_table[0, m], 1.0)

    own_diagonal = jnp.where(sub < 6, near_table[0, member], 1.0)

    def source_row(step, chunk, c):
        at = 3 * (chunk % 2) + c
        return near_table[step, chunk // 2, at : at + 1, :]

    def coarse_sweep(step):
        for h in range(2):
            total = [zero] * 3
            for k in range(4):
                rows = 32 * h + 8 * k
                where = coarse_place[rows : rows + 8, :]
                lane, chunk = where & (LANES - 1), where >> 7
                near = [zero] * 3
                for n in range(2 * MEMBERS):
                    mine = chunk == n
                    for c in range(3):
                        near[c] = jnp.where(mine, pick(spread(source_row(step, n, c)), lane), near[c])
                for i in range(3):
                    for c in range(3):
                        total[i] = total[i] + coarse_block[3 * i + c, rows : rows + 8, :] * near[c]
            for i in range(3):
                tile[3 * h + i : 3 * h + i + 1, :] = jnp.sum(total[i], axis=0, keepdims=True)
        old = near_table[step, member]
        pull = jnp.where(sub < 6, tile[...], 0.0)
        return old + damping * (rhs[member] - (own_diagonal * old - pull)) / own_diagonal

    def sweep(step, carry):
        near_table[step + 1, member] = coarse_sweep(step)
        send_near(step + 1)
        wait_near(step + 1, near_recv)
        return carry

    lax.fori_loop(2, 2 + CSWEEPS - 1, sweep, 0)
    last = 1 + CSWEEPS

    mine = near_table[last, member]
    mine = jnp.where(block >= 4, pltpu.roll(mine, 5, 0), mine)
    quarter = block & 3
    shown = mine
    for jj in range(1, 4):
        shown = jnp.where(quarter == jj, pltpu.roll(mine, LANES - 32 * jj, 1), shown)
    correction_ref[...] = shown[0:3, 0:32]

    where_own = node_place[...].astype(jnp.int32)
    where_halo = jnp.concatenate([halo_in[0, 24:28, :], halo_in[1, 24:28, :]], axis=0).astype(jnp.int32)
    lane_own, chunk_own = where_own & (LANES - 1), where_own >> 7
    lane_halo, chunk_halo = where_halo & (LANES - 1), where_halo >> 7
    add_own, add_halo = [zero] * 3, [zero] * 3
    for n in range(2 * MEMBERS):
        for c in range(3):
            source = spread(source_row(last, n, c))
            add_own[c] = jnp.where(chunk_own == n, pick(source, lane_own), add_own[c])
            add_halo[c] = jnp.where(chunk_halo == n, pick(source, lane_halo), add_halo[c])
    wait_halo(3)
    for c in range(3):
        second[c, 0:2, :] = edge_in[0, 2 * c : 2 * c + 2, :]
        second[c, 14:16, :] = edge_in[1, 2 * c : 2 * c + 2, :]
        third[c, 4:12, :] = second[c, 4:12, :] + add_own[c]
        third[c, 0:4, :] = second[c, 0:4, :] + add_halo[c][0:4]
        third[c, 12:16, :] = second[c, 12:16, :] + add_halo[c][4:8]

    apply_fine(third, range(-2, 10))
    smooth(third, fourth, -2, 10)
    apply_fine(fourth, range(8))
    for c in range(3):
        value = fourth[c, 4:12, :] + damping * residual_of(fourth, c, 0, 8) / diagonal[c, 4:12, :]
        for j in range(8):
            out_ref[c : c + 1, j * LANES : (j + 1) * LANES] = value[j : j + 1]

    for step in range(4):
        close_halo(step)
    wait_far(far_table, 0, far_send)
    wait_far(far_sums, 1, far_send)
    for step in range(2):
        wait_near(step, near_send)

    def drain(step, carry):
        wait_near(step, near_send)
        return carry

    lax.fori_loop(3, 2 + CSWEEPS, drain, 0)


def finish(field_ref, correction_ref, out_field_ref, out_correction_ref):
    out_field_ref[...] = field_ref[...]
    out_correction_ref[...] = correction_ref[...]


def per_device(
    right_side,
    fine_diagonal,
    fine_columns,
    fine_blocks,
    aggregate_of_node,
    coarse_row_of_aggregate,
    coarse_diagonal,
    coarse_columns,
    coarse_blocks,
):
    nodes = right_side.shape[0]
    own = coarse_diagonal.shape[0]
    steps = 2 + CSWEEPS
    f32 = jnp.float32
    i32 = jnp.int32
    vmem = pl.BlockSpec(memory_space=pltpu.VMEM)
    anywhere = pl.BlockSpec(memory_space=pl.ANY)
    shapes = (jax.ShapeDtypeStruct((3, nodes), f32), jax.ShapeDtypeStruct((3, own), f32))
    operands = (
        right_side.T,
        fine_diagonal.T,
        fine_columns.T,
        jnp.transpose(fine_blocks, (2, 3, 1, 0)),
        aggregate_of_node.reshape(8, LANES),
        coarse_row_of_aggregate.reshape(1, own),
        coarse_diagonal.T,
        coarse_columns,
        jnp.transpose(coarse_blocks, (2, 3, 0, 1)),
    )
    tall = pltpu.VMEM((3, 16, LANES), f32)
    outs = pl.pallas_call(
        kernel,
        out_shape=shapes,
        in_specs=[anywhere] * 9,
        out_specs=(vmem, vmem),
        scratch_shapes=[pltpu.VMEM(operand.shape, operand.dtype) for operand in operands]
        + [
            tall,
            tall,
            pltpu.VMEM((32, 12 * LANES), i32),
            tall,
            tall,
            tall,
            tall,
            tall,
            pltpu.VMEM((2, 32, LANES), f32),
            pltpu.VMEM((2, 32, LANES), f32),
            pltpu.VMEM((8, LANES), f32),
            pltpu.VMEM((2, 8, LANES), f32),
            pltpu.VMEM((2, 8, LANES), f32),
            pltpu.VMEM((2, 3, 3, 27, WIN), f32),
            pltpu.VMEM((2, 27, WIN), i32),
            pltpu.VMEM((384, LANES), f32),
            pltpu.VMEM((16, LANES), f32),
            pltpu.VMEM((BLOCKS, 96, LANES), f32),
            pltpu.VMEM((BLOCKS, 1, LANES), f32),
            pltpu.VMEM((steps, MEMBERS, 8, LANES), f32),
            pltpu.VMEM((9, 64, LANES), f32),
            pltpu.VMEM((64, LANES), i32),
            pltpu.VMEM((32, LANES), i32),
            pltpu.VMEM((32, LANES), i32),
            pltpu.VMEM((MEMBERS, 8, LANES), f32),
            pltpu.VMEM((8, LANES), f32),
            pltpu.SemaphoreType.DMA((9,)),
            pltpu.SemaphoreType.DMA((4, 2)),
            pltpu.SemaphoreType.DMA((4, 2)),
            pltpu.SemaphoreType.DMA((2,)),
            pltpu.SemaphoreType.DMA((2,)),
            pltpu.SemaphoreType.DMA((steps,)),
            pltpu.SemaphoreType.DMA((steps,)),
        ],
        compiler_params=pltpu.CompilerParams(collective_id=0, has_side_effects=True),
    )(*operands)
    field, correction = pl.pallas_call(finish, out_shape=shapes, in_specs=[vmem] * 2, out_specs=(vmem, vmem))(*outs)
    return (field.T, correction.T)


def solution(mesh):
    return jax.shard_map(
        per_device,
        mesh=mesh,
        in_specs=(
            P("dom", None),
            P("dom", None),
            P("dom", None),
            P("dom", None, None, None),
            P("dom"),
            P("dom"),
            P("dom", None),
            P("dom", None),
            P("dom", None, None, None),
        ),
        out_specs=(P("dom", None), P("dom", None)),
        check_vma=False,
    )
```

time: 67.4 us -> 57.7 us (0.86); the launches traced: 67.2 us -> 56.7 us
  Pallas kernels: 64 us -> 56 us
  local copies, waits for them, and re-layouts: 2.56 us -> 0 us
    pallas_call x1 -> x2, Pallas kernels: 64 us -> 56 us  [the longest x1 54.7 us: per_device(): pl.pallas_call(kernel, out_shape=shapes, in_specs=[anywhere] * 9, out_spe...]
    unnamed x2 -> x0, local copies, waits for them, and re-layouts: 2.56 us -> none
where the time goes in v2:
time: 57.7 us; the launch traced here: 56.7 us
  Pallas kernels  56 us (97%)
  between operations  0.64 us (1%)
    pallas_call x1, Pallas kernels, per_device(): pl.pallas_call(kernel, out_shape=shapes, in_specs=[anywhere] * 9, out_spe...  54.7 us
    pallas_call x1, Pallas kernels, per_device(): pl.pallas_call(finish, out_shape=shapes, in_specs=[vmem] * 2, out_specs=(...  1.33 us

profile of v2, /device:TPU:0, one launch (start us, length us, event | category | flops | bytes accessed | tf_op | source)
XLA Modules:
  0.0 56.7 jit_solution(14628519114548392284)
XLA Ops:
  0.6 54.7 %shard_map.104 = (f32[3,1024]{1,0:T(4,128)}, f32[3,32]{1,0:T(4,128)}) custom-call(f32[3,1024]{1,0:T(4,128)} %bitcast.13, f32[3,1024]{1,0:T(4,128)} %bitcast.14, s32[27,1024]{1,0:T(8,128)} %bitcast.12, f32[3,3,27,1024]{3,2,1,0:T(8,128)} %bitcast.10, s32[8,128]{1,0:T(8,128)} %bitcast.15, s32[1,32]{1,0:T(1,128)} %bitcast.17, f32[3,32]{1,0:T(4,128)} %bitcast.16, ...), custom_call_target="tpu_custom_call" | custom-call | tf_op jit(solution)/shard_map/pallas_call | solution.py:503
  55.3 1.3 %shard_map.105 = (f32[3,1024]{1,0:T(4,128)}, f32[3,32]{1,0:T(4,128)}) custom-call(f32[3,1024]{1,0:T(4,128)} %get-tuple-element.6.field_ref, f32[3,32]{1,0:T(4,128)} %get-tuple-element.7.correction_ref), custom_call_target="tpu_custom_call" | custom-call | tf_op jit(solution)/shard_map/pallas_call | solution.py:546
